TPU v7x, 512 devices: a 8x2x16 block of a 8x8x16 slice. The times are simulated.
512 devices in a mesh: groups: 2 (over y), users: 16 (over z), routers: 8 (over x), heads: 2 (over core).
Axes of the slice: x: 8, y: 2, z: 16, core: 2. Of those that a mesh axis runs over, the one named last changes fastest.
The devices are a block of a 8x8x16 slice.
Arguments:
- items: bfloat16 [4096, 64, 1024], P(('groups', 'users', 'routers')), parts along dimension 0, may hold values from -6 to 6
- block_owner: int32 [4096, 1], P(('groups', 'users', 'routers')), parts along dimension 0, may hold values from 0 to 15; in each aligned block of 16 rows (0 to 15, 16 to 31, ...) at most 2 rows name the same one
- block_user: int32 [4096], P(('groups', 'users', 'routers')), parts along dimension 0, may hold values from 0 to 1
- block_fill: int32 [4096], P(('groups', 'users', 'routers')), parts along dimension 0, may hold values from 1 to 64
- prefix_keys: bfloat16 [64, 256, 1024], P(('groups', 'users'), None, 'heads'), parts along dimension 0, may hold values from -6 to 6
- prefix_values: bfloat16 [64, 256, 1024], P(('groups', 'users'), None, 'heads'), parts along dimension 0, may hold values from -6 to 6
- w_in: bfloat16 [4, 1024, 1024], P(None, 'routers', 'heads'), may hold values from -0.1875 to 0.1875
- attn_gain: bfloat16 [1024], P('heads'), may hold values from 0.25 to 1.75
- w_o: bfloat16 [1024, 1024], P('heads', 'routers'), may hold values from -0.1875 to 0.1875
- mlp_gain: bfloat16 [1024], replicated, may hold values from 0.25 to 1.75
- w_one: bfloat16 [1024, 256], replicated, may hold values from -0.1875 to 0.1875
- w_two: bfloat16 [256], replicated, may hold values from -0.375 to 0.375
Outputs:
- scores: float32 [4096, 64], P(('groups', 'users', 'routers')), parts along dimension 0
There are 2 independent parts, one for each index of `groups`. A program takes and returns all parts, laid end to end along the dimension named above; an argument that names none is the same for every part. Nothing has to cross between parts.
Inputs may be any that keep to these rules, and one draw needn't show every extreme that they name: `block_owner`: within the rows of one device (aligned blocks of 16 blocks), no owner is named by more than 2 rows, and in every draw some owner is named by exactly 2 rows of some device.
All inputs are finite; a program needn't handle non-finite values.
Results may differ from a plain program's by a relative error of at most 0.005.
Values may be sent and summed in bfloat16 or wider, within the bound.
No kernel may reach another device: no remote copies, remote signals or barrier semaphores. Data moves between devices by JAX's collectives and lax.ppermute only.
A program may use at most 64 MiB of HBM per device.

v0:
```python
import jax
import jax.numpy as jnp
from jax import lax
from jax.sharding import PartitionSpec as P

D = 1024
HEAD_DIM = 128
CAP = 2
HD = 1024
EPSILON = 1e-05


def items_in_groups(x, axis, split_dim, concat_dim, work, item_dim, out_dim):

    def moved(group):
        return lax.all_to_all(group, axis, split_axis=split_dim, concat_axis=concat_dim, tiled=True)

    items = jax.tree.leaves(x)[0].shape[item_dim]
    ends = [items * k // 2 for k in range(2 + 1)] if items % 2 == 0 else [0, items]
    groups = [
        jax.tree.map(lambda a: lax.slice_in_dim(a, low, high, axis=item_dim), x)
        for low, high in zip(ends, ends[1:])
    ]
    arrived = [moved(group) for group in groups]
    made = [work(group) for group in arrived]
    return jax.tree.map(lambda *parts: jnp.concatenate(parts, axis=out_dim), *made)


def in_blocks(x, dim, peers):
    shape = x.shape
    tiles = x.reshape(*shape[:dim], peers, shape[dim] // peers, *shape[dim + 1 :])
    return jnp.moveaxis(tiles, dim, 0)


def sent_and_summed(x, axis, dim):
    tiles = in_blocks(x, dim, lax.axis_size(axis))
    arrived = lax.all_to_all(tiles, axis, split_axis=0, concat_axis=0, tiled=True)
    return arrived.sum(axis=0)


def sent_to_all(x, axis):
    copies = jnp.broadcast_to(x, (lax.axis_size(axis), *x.shape))
    return lax.all_to_all(copies, axis, split_axis=0, concat_axis=0, tiled=True)


def taken_together(x, axis):
    return sent_to_all(x, axis).sum(axis=0)


def prefix_attention(group_queries, group_users, prefix_keys, prefix_values):
    group_size, block_width, half_width = group_queries.shape
    heads_here = half_width // HEAD_DIM
    safe_user = jnp.maximum(group_users, 0)
    user_keys = jnp.take(prefix_keys, safe_user, axis=0)
    user_values = jnp.take(prefix_values, safe_user, axis=0)
    query_heads = group_queries.reshape(group_size, block_width, heads_here, HEAD_DIM)
    key_heads = user_keys.reshape(group_size, -1, heads_here, HEAD_DIM)
    value_heads = user_values.reshape(group_size, -1, heads_here, HEAD_DIM)
    raw_scores = jnp.einsum(
        "gqhd,gkhd->ghqk", query_heads, key_heads, preferred_element_type=jnp.float32
    ) * HEAD_DIM ** (-0.5)
    weights = jax.nn.silu(raw_scores).astype(jnp.bfloat16)
    summed = jnp.einsum("ghqk,gkhd->gqhd", weights, value_heads, preferred_element_type=jnp.float32)
    return summed.reshape(group_size, block_width, half_width).astype(jnp.bfloat16)


def local(
    items,
    block_owner,
    block_user,
    block_fill,
    prefix_keys,
    prefix_values,
    w_in,
    attn_gain,
    w_o,
    mlp_gain,
    w_one,
    w_two,
):
    blocks, block_width, model_width = items.shape
    row_count = blocks * block_width
    half_width = w_in.shape[2]
    heads_here = half_width // HEAD_DIM
    peer_count = lax.axis_size("users")
    slot_count = peer_count * CAP
    score_scale = HEAD_DIM ** (-0.5)
    flat_items = items.reshape(row_count, model_width)
    projected = jnp.einsum(
        "rk,pkc->prc",
        flat_items,
        lax.all_gather(w_in, "routers", axis=1, tiled=True),
        preferred_element_type=jnp.float32,
    )
    activated = jax.nn.silu(projected)
    queries = activated[0].astype(jnp.bfloat16)
    target = block_owner[:, 0]
    earlier = lax.broadcasted_iota(jnp.int32, (blocks, blocks), 1) < lax.broadcasted_iota(
        jnp.int32, (blocks, blocks), 0
    )
    same_target = target[:, None] == target[None, :]
    dest_rank = jnp.sum((same_target & earlier).astype(jnp.int32), axis=1)
    position = target * CAP + dest_rank
    selector = lax.broadcasted_iota(jnp.int32, (slot_count, blocks), 0) == position[None, :]
    block_queries = queries.reshape(blocks, block_width * half_width)
    outgoing = jnp.dot(
        selector.astype(jnp.bfloat16), block_queries, preferred_element_type=jnp.float32
    ).astype(jnp.bfloat16)
    outgoing = outgoing.reshape(peer_count, CAP, block_width, half_width)
    slot_user = jnp.sum(jnp.where(selector, block_user[None, :] + 1, 0), axis=1) - 1
    slot_user = slot_user.reshape(peer_count, CAP)

    def serve_slots(received):
        arrived, arrived_users = received
        sources, per_source = arrived_users.shape
        total_slots = sources * per_source
        flat_queries = arrived.reshape(total_slots, block_width, half_width)
        flat_users = arrived_users.reshape(total_slots)
        packing = jnp.argsort((flat_users < 0).astype(jnp.int32), stable=True)
        used_slots = jnp.sum((flat_users >= 0).astype(jnp.int32))
        packed_queries = jnp.take(flat_queries, packing, axis=0)
        packed_users = jnp.take(flat_users, packing, axis=0)
        needed = (used_slots + 3) // 4

        def attend_group(group_index, buffer):
            first_slot = group_index * 4
            group_queries = lax.dynamic_slice_in_dim(packed_queries, first_slot, 4, 0)
            group_users = lax.dynamic_slice_in_dim(packed_users, first_slot, 4, 0)
            result = prefix_attention(group_queries, group_users, prefix_keys, prefix_values)
            return lax.dynamic_update_slice_in_dim(buffer, result, first_slot, 0)

        packed_out = lax.fori_loop(
            0, needed, attend_group, jnp.zeros((total_slots, block_width, half_width), jnp.bfloat16)
        )
        inverse = jnp.argsort(packing)
        attended_slots = jnp.take(packed_out, inverse, axis=0)
        return lax.all_to_all(
            attended_slots.reshape(sources, per_source, block_width, half_width),
            "users",
            split_axis=0,
            concat_axis=0,
            tiled=True,
        )

    returned = items_in_groups((outgoing, slot_user), "users", 0, 0, serve_slots, 1, 1)
    prefix_part = jnp.take(returned.reshape(slot_count, block_width * half_width), position, axis=0)
    prefix_part = prefix_part.reshape(row_count, heads_here, HEAD_DIM).astype(jnp.float32)
    query_heads = queries.astype(jnp.float32).reshape(row_count, heads_here, HEAD_DIM)
    self_keys = activated[1].reshape(row_count, heads_here, HEAD_DIM)
    self_values = activated[2].reshape(row_count, heads_here, HEAD_DIM)
    own_term = (
        jax.nn.silu(jnp.sum(query_heads * self_keys, axis=-1) * score_scale)[..., None]
        * self_values
    )
    attended = (prefix_part + own_term).reshape(row_count, half_width)
    totals = lax.psum((jnp.sum(attended, axis=1), jnp.sum(attended * attended, axis=1)), "heads")
    row_mean = totals[0] / HD
    row_var = totals[1] / HD - row_mean * row_mean
    gated = (
        (attended - row_mean[:, None])
        * lax.rsqrt(row_var + EPSILON)[:, None]
        * attn_gain.astype(jnp.float32)
        * activated[3]
    ).astype(jnp.bfloat16)
    partial_out = jnp.dot(
        gated,
        lax.all_gather(w_o, "routers", axis=1, tiled=True),
        preferred_element_type=jnp.float32,
    )
    head_share = sent_and_summed(partial_out, "heads", 1)
    share_cols = head_share.shape[1]
    offset = lax.axis_index("heads") * share_cols
    residual = (
        lax.dynamic_slice_in_dim(flat_items, offset, share_cols, 1).astype(jnp.float32) + head_share
    )
    squares = lax.psum(jnp.sum(residual * residual, axis=1), "heads")
    row_scale = lax.rsqrt(squares / D + EPSILON)
    gain_part = lax.dynamic_slice_in_dim(mlp_gain, offset, share_cols, 0)
    normed = (residual * row_scale[:, None] * gain_part.astype(jnp.float32)).astype(jnp.bfloat16)
    weight_part = lax.dynamic_slice_in_dim(w_one, offset, share_cols, 0)
    inner_sum = taken_together(
        jnp.dot(normed, weight_part, preferred_element_type=jnp.float32), "heads"
    )
    hidden = jax.nn.silu(inner_sum).astype(jnp.bfloat16)
    block_scores = jnp.dot(hidden, w_two, preferred_element_type=jnp.float32).reshape(
        blocks, block_width
    )
    is_valid = lax.broadcasted_iota(jnp.int32, (blocks, block_width), 1) < block_fill[:, None]
    return jnp.where(is_valid, block_scores, jnp.zeros_like(block_scores))


def solution(mesh):
    placed = (
        P(("groups", "users", "routers"), None, None),
        P(("groups", "users", "routers"), None),
        P(("groups", "users", "routers")),
        P(("groups", "users", "routers")),
        P(("groups", "users"), None, "heads"),
        P(("groups", "users"), None, "heads"),
        P(None, "routers", "heads"),
        P("heads"),
        P("heads", "routers"),
        P(),
        P(),
        P(),
    )
    return jax.shard_map(
        local,
        mesh=mesh,
        in_specs=placed,
        out_specs=P(("groups", "users", "routers"), None),
        check_vma=False,
    )
```

profile of v0, /device:TPU:65, one launch (start us, length us, event | category | flops | bytes accessed | tf_op | source)
XLA Modules:
  0.0 428.9 jit_solution(11410321025123503344)
XLA Ops:
  6.6 2.1 copy.77
  11.2 44.2 %all-to-all-start.3 = ((s32[16,1,1]{2,1,0:T(1,128)}), s32[16,1,1]{2,1,0:T(1,128)S(1)}, u32[]{:S(2)}, u32[]{:S(2)}) async-start(s32[16,1,1]{2,1,0:T(1,128)} %bitcast.11), calls=%async_computation.3 | async-start | bytes 16384 | tf_op jit(solution)/shard_map/all_to_all | solution.py:16
  55.4 55.9 %all-gather.3.cloned.1.call-done = bf16[4,1024,512]{1,2,0:T(8,128)(2,1)} async-done(((bf16[4,128,512]{1,2,0:T(8,128)(2,1)}), bf16[4,1024,512]{1,2,0:T(8,128)(2,1)}) %all-gather.3.cloned.1.call-update) | async-done | bytes 4194320 | tf_op jit(solution)/shard_map/all_gather | solution.py:92
  111.3 7.8 %bitcast_multiply_fusion = f32[4,1024,512]{1,2,0:T(8,128)S(1)} fusion(bf16[4,1024,512]{1,2,0:T(8,128)(2,1)} %all-gather.3.cloned.1.call-done, bf16[1024,1024,1]{1,0,2:T(8,128)(2,1)} %bitcast.171), kind=kOutput, calls=%fused_computation.54 | convolution fusion | flops 4303355904 | bytes 14680064 | tf_op jit(solution)/shard_map/rk,pkc->prc/dot_general | solution.py:89
  119.1 3.2 copy-done.3
  122.4 1.9 slice_multiply_fusion.1
  126.9 9.9 %all-to-all-start = ((s32[16,1,1]{2,1,0:T(1,128)}), s32[16,1,1]{2,1,0:T(1,128)S(1)}, u32[]{:S(2)}, u32[]{:S(2)}) async-start(s32[16,1,1]{2,1,0:T(1,128)} %bitcast.6), calls=%async_computation | async-start | bytes 16384 | tf_op jit(solution)/shard_map/all_to_all | solution.py:16
  136.8 1.5 fusion.58
  138.2 9.6 %all-to-all-done = s32[16,1,1]{2,1,0:T(1,128)S(1)} async-done(((s32[16,1,1]{2,1,0:T(1,128)}), s32[16,1,1]{2,1,0:T(1,128)S(1)}, u32[]{:S(2)}, u32[]{:S(2)}) %all-to-all-start) | async-done | bytes 96 | tf_op jit(solution)/shard_map/all_to_all | solution.py:16
  147.8 4.1 all-to-all-start.4
  161.9 35.7 %all-to-all-done.4 = bf16[16,1,64,512]{3,2,1,0:T(8,128)(2,1)S(1)} async-done(((bf16[16,1,64,512]{3,2,1,0:T(8,128)(2,1)}), bf16[16,1,64,512]{3,2,1,0:T(8,128)(2,1)S(1)}, u32[]{:S(2)}, u32[]{:S(2)}) %all-to-all-start.4) | async-done | bytes 1048608 | tf_op jit(solution)/shard_map/all_to_all | solution.py:16
  197.6 10.8 %all-to-all-start.1 = ((bf16[16,1,64,512]{3,2,1,0:T(8,128)(2,1)}), bf16[16,1,64,512]{3,2,1,0:T(8,128)(2,1)}, u32[]{:S(2)}, u32[]{:S(2)}) async-start(bf16[16,1,64,512]{3,2,1,0:T(8,128)(2,1)} %get-tuple-element.142), calls=%async_computation.1 | async-start | bytes 2097152 | tf_op jit(solution)/shard_map/all_to_all | solution.py:16
  208.4 1.8 gather_fusion.9
  212.6 1.8 gather_fusion.10
  215.5 37.3 %all-to-all-done.1 = bf16[16,1,64,512]{3,2,1,0:T(8,128)(2,1)} async-done(((bf16[16,1,64,512]{3,2,1,0:T(8,128)(2,1)}), bf16[16,1,64,512]{3,2,1,0:T(8,128)(2,1)}, u32[]{:S(2)}, u32[]{:S(2)}) %all-to-all-start.1) | async-done | bytes 1048608 | tf_op jit(solution)/shard_map/all_to_all | solution.py:16
  252.8 13.8 %all-to-all-start.5 = ((bf16[16,1,64,512]{3,2,1,0:T(8,128)(2,1)}), bf16[16,1,64,512]{3,2,1,0:T(8,128)(2,1)}, u32[]{:S(2)}, u32[]{:S(2)}) async-start(bf16[16,1,64,512]{3,2,1,0:T(8,128)(2,1)} %select_bitcast_fusion.4), calls=%async_computation.5 | async-start | bytes 2097152 | tf_op jit(solution)/shard_map/all_to_all | solution.py:137
  266.6 1.8 gather_fusion.6
  270.7 24.7 %while.20 = (s32[]{:T(128)}, bf16[16,64,512]{2,1,0:T(8,128)(2,1)}, s32[]{:T(128)}, s32[16]{0:T(128)S(1)}, bf16[2,256,512]{2,1,0:T(8,128)(2,1)S(1)}, /*index=5*/b...) while((s32[]{:T(128)}, bf16[16,64,512]{2,1,0:T(8,128)(2,1)}, ...), condition=%wide.region_5.9_spmd, body=%wide.region_4.8_spmd.sunk | while | flops 136971280 | bytes 11538695 | solution.py:132
  271.4 1.6 gather_fusion.1
  273.0 2.8 select_bitcast_fusion.8
  275.8 2.4 fusion.76
  279.7 1.6 gather_fusion.1
  281.3 2.8 select_bitcast_fusion.8
  284.0 2.4 fusion.76
  287.9 1.6 gather_fusion.1
  289.5 2.8 select_bitcast_fusion.8
  292.3 2.4 fusion.76
  295.4 1.8 gather_fusion.7
  298.4 13.3 %all-to-all-done.5 = bf16[16,1,64,512]{3,2,1,0:T(8,128)(2,1)} async-done(((bf16[16,1,64,512]{3,2,1,0:T(8,128)(2,1)}), bf16[16,1,64,512]{3,2,1,0:T(8,128)(2,1)}, u32[]{:S(2)}, u32[]{:S(2)}) %all-to-all-start.5) | async-done | bytes 1048608 | tf_op jit(solution)/shard_map/all_to_all | solution.py:137
  311.8 13.0 %all-to-all-start.2 = ((bf16[16,1,64,512]{3,2,1,0:T(8,128)(2,1)}), bf16[16,1,64,512]{3,2,1,0:T(8,128)(2,1)}, u32[]{:S(2)}, u32[]{:S(2)}) async-start(bf16[16,1,64,512]{3,2,1,0:T(8,128)(2,1)} %select_bitcast_fusion.5), calls=%async_computation.2 | async-start | bytes 2097152 | tf_op jit(solution)/shard_map/all_to_all | solution.py:137
  325.9 41.3 %all-gather.5.cloned.1.call-done = bf16[512,1024]{1,0:T(8,128)(2,1)} async-done(((bf16[512,128]{1,0:T(8,128)(2,1)}), bf16[512,1024]{1,0:T(8,128)(2,1)}) %all-gather.5.cloned.1.call-update) | async-done | bytes 1048592 | tf_op jit(solution)/shard_map/all_gather | solution.py:167
  367.2 2.3 copy.82
  369.9 1.7 pad_maximum_fusion
  372.9 2.2 gather_fusion.4
  375.1 2.5 gather.19
  378.9 1.5 copy.81
  380.3 1.5 copy.80
  381.8 2.1 fusion.43
  383.9 7.8 %all-reduce = (f32[1024]{0:T(1024)S(1)}, f32[1024]{0:T(1024)S(1)}) all-reduce(f32[1024]{0:T(1024)S(1)} %get-tuple-element.95, f32[1024]{0:T(1024)S(1)} %get-tuple-element.94), channel_id=1, replica_groups=mesh['groups'=2,'users'=16,'routers'=8,'heads'=2] {'heads'}, use_global_device_ids=true, to_apply=%region_16.20 | all-reduce | flops 2048 | bytes 16384 | tf_op jit(solution)/shard_map/psum | solution.py:156
  391.8 2.9 fusion.37
  394.7 1.3 convolution_bitcast_fusion
  396.0 8.2 %all_to_all.48 = f32[2,1024,512]{2,1,0:T(8,128)} all-to-all(f32[2,1024,512]{2,1,0:T(8,128)S(1)} %convolution_bitcast_fusion), channel_id=1, replica_groups=mesh['groups'=2,'users'=16,'routers'=8,'heads'=2] {'heads'}, dimensions={0} | all-to-all | bytes 8388608 | tf_op jit(solution)/shard_map/all_to_all | solution.py:37
  404.1 2.9 reduce_sum.100
  407.0 1.6 multiply_reduce_fusion
  408.6 2.6 psum.23
  411.1 1.7 fusion.44
  413.0 5.4 %all_to_all.49 = f32[2,1024,256]{2,1,0:T(8,128)S(1)} all-to-all(f32[2,1024,256]{2,1,0:T(8,128)S(1)} %broadcast_in_dim.74), channel_id=1, replica_groups=mesh['groups'=2,'users'=16,'routers'=8,'heads'=2] {'heads'}, dimensions={0} | all-to-all | bytes 4194304 | tf_op jit(solution)/shard_map/all_to_all | solution.py:43
  419.7 1.6 fusion.49
  (105 shorter events, 30.9 us)
Async XLA Ops:
  6.5 404.6 %copy-start = (bf16[1024,256]{1,0:T(8,128)(2,1)S(1)}, bf16[1024,256]{1,0:T(8,128)(2,1)}, u32[]{:S(2)}) copy-start(bf16[1024,256]{1,0:T(8,128)(2,1)} %param.32) | copy-start | bytes 1572868
  6.6 104.8 %all-gather.3.cloned.1.call-start = ((), (), s32[]{:S(2)}) async-start(), calls=%async_computation.8 | async-start | bytes 4718592 | tf_op jit(solution)/shard_map/all_gather | solution.py:92
  11.2 115.7 %all-to-all-start.3 = ((s32[16,1,1]{2,1,0:T(1,128)}), s32[16,1,1]{2,1,0:T(1,128)S(1)}, u32[]{:S(2)}, u32[]{:S(2)}) async-start(s32[16,1,1]{2,1,0:T(1,128)} %bitcast.11), calls=%async_computation.3 | async-start | bytes 16384 | tf_op jit(solution)/shard_map/all_to_all | solution.py:16
  119.1 3.2 copy-start.3
  126.9 20.9 %all-to-all-start = ((s32[16,1,1]{2,1,0:T(1,128)}), s32[16,1,1]{2,1,0:T(1,128)S(1)}, u32[]{:S(2)}, u32[]{:S(2)}) async-start(s32[16,1,1]{2,1,0:T(1,128)} %bitcast.6), calls=%async_computation | async-start | bytes 16384 | tf_op jit(solution)/shard_map/all_to_all | solution.py:16
  147.8 49.8 %all-to-all-start.4 = ((bf16[16,1,64,512]{3,2,1,0:T(8,128)(2,1)}), bf16[16,1,64,512]{3,2,1,0:T(8,128)(2,1)S(1)}, u32[]{:S(2)}, u32[]{:S(2)}) async-start(bf16[16,1,64,512]{3,2,1,0:T(8,128)(2,1)} %get-tuple-element.143), calls=%async_computation.4 | async-start | bytes 2097152 | tf_op jit(solution)/shard_map/all_to_all | solution.py:16
  197.6 10.8 %copy-start.6 = (bf16[16,1,64,512]{3,2,1,0:T(8,128)(2,1)}, bf16[16,1,64,512]{3,2,1,0:T(8,128)(2,1)S(1)}, u32[]{:S(2)}) copy-start(bf16[16,1,64,512]{3,2,1,0:T(8,128)(2,1)S(1)} %all-to-all-done.4) | copy-start | bytes 3145732
  197.6 55.2 %all-to-all-start.1 = ((bf16[16,1,64,512]{3,2,1,0:T(8,128)(2,1)}), bf16[16,1,64,512]{3,2,1,0:T(8,128)(2,1)}, u32[]{:S(2)}, u32[]{:S(2)}) async-start(bf16[16,1,64,512]{3,2,1,0:T(8,128)(2,1)} %get-tuple-element.142), calls=%async_computation.1 | async-start | bytes 2097152 | tf_op jit(solution)/shard_map/all_to_all | solution.py:16
  210.3 2.3 copy-start.1
  210.3 2.2 copy-start.2
  252.8 58.9 %all-to-all-start.5 = ((bf16[16,1,64,512]{3,2,1,0:T(8,128)(2,1)}), bf16[16,1,64,512]{3,2,1,0:T(8,128)(2,1)}, u32[]{:S(2)}, u32[]{:S(2)}) async-start(bf16[16,1,64,512]{3,2,1,0:T(8,128)(2,1)} %select_bitcast_fusion.4), calls=%async_computation.5 | async-start | bytes 2097152 | tf_op jit(solution)/shard_map/all_to_all | solution.py:137
  297.2 28.3 %copy-start.12 = (bf16[256]{0:T(256)(128)(2,1)S(1)}, bf16[256]{0:T(256)(128)(2,1)}, u32[]{:S(2)}) copy-start(bf16[256]{0:T(256)(128)(2,1)} %param.33) | copy-start | bytes 1540
  297.2 28.4 %copy-start.9 = (bf16[512]{0:T(512)(128)(2,1)S(1)}, bf16[512]{0:T(512)(128)(2,1)}, u32[]{:S(2)}) copy-start(bf16[512]{0:T(512)(128)(2,1)} %param.29) | copy-start | bytes 3076
  297.3 28.4 %copy-start.8 = (s32[16,1]{0,1:T(1,128)S(1)}, s32[16,1]{0,1:T(1,128)}, u32[]{:S(2)}) copy-start(s32[16,1]{0,1:T(1,128)} %param.23) | copy-start | bytes 196
  297.3 28.5 %copy-start.10 = (bf16[1024]{0:T(1024)(128)(2,1)S(1)}, bf16[1024]{0:T(1024)(128)(2,1)}, u32[]{:S(2)}) copy-start(bf16[1024]{0:T(1024)(128)(2,1)} %param.31) | copy-start | bytes 6148
  298.4 71.1 %copy-start.5 = (f32[1,1024,512]{1,2,0:T(8,128)S(1)}, f32[1,1024,512]{1,2,0:T(8,128)}, u32[]{:S(2)}) copy-start(f32[1,1024,512]{1,2,0:T(8,128)} %get-tuple-element.136) | copy-start | bytes 6291460
  311.8 58.2 %all-to-all-start.2 = ((bf16[16,1,64,512]{3,2,1,0:T(8,128)(2,1)}), bf16[16,1,64,512]{3,2,1,0:T(8,128)(2,1)}, u32[]{:S(2)}, u32[]{:S(2)}) async-start(bf16[16,1,64,512]{3,2,1,0:T(8,128)(2,1)} %select_bitcast_fusion.5), calls=%async_computation.2 | async-start | bytes 2097152 | tf_op jit(solution)/shard_map/all_to_all | solution.py:137
  324.8 42.4 %all-gather.5.cloned.1.call-start = ((), (), s32[]{:S(2)}) async-start(), calls=%async_computation.9 | async-start | bytes 1179648 | tf_op jit(solution)/shard_map/all_gather | solution.py:167
  375.1 2.5 copy-start.4
  391.8 2.9 copy-start.7
  419.7 1.7 copy-start.11
Sparse Core Ops, SparseCore 0:
  9.4 101.9 all-gather.2
  327.6 39.5 all-gather.4
where the time goes:
time: 431 us; the launch traced here: 429 us
  waiting for transfers between devices  194 us (45%)
  starting transfers between devices  95.8 us (22%)
  local copies, waits for them, and re-layouts  41.8 us (10%)
  other arithmetic  37.5 us (9%)
  blocking collectives  23.9 us (6%)
  matrix products  20.5 us (5%)
  between operations  15.1 us (4%)
    all_to_all x4, waiting for transfers between devices, moved(): lax.all_to_all(group, axis, split_axis=split_dim, concat_axis=concat_dim,...  82.6 us
    all_to_all x4, starting transfers between devices, moved(): lax.all_to_all(group, axis, split_axis=split_dim, concat_axis=concat_dim,...  69 us
    all_gather x1, waiting for transfers between devices, local(): lax.all_gather(w_in, 'routers', axis=1, tiled=True)  55.9 us
    all_gather x1, waiting for transfers between devices, local(): lax.all_gather(w_o, 'routers', axis=1, tiled=True)  41.3 us
    all_to_all x2, starting transfers between devices, serve_slots(): lax.all_to_all(attended_slots.reshape(sources, per_source, block_width, h...  26.7 us
    all_to_all x2, waiting for transfers between devices, serve_slots(): lax.all_to_all(attended_slots.reshape(sources, per_source, block_width, h...  13.6 us
    gather x5, local copies, waits for them, and re-layouts, local(): jnp.take(returned.reshape(slot_count, block_width * half_width), position...  8.96 us
  transfers between devices with their start and end apart: 8, of which 7 were waited for; matrix products, arithmetic and copies ran while one was open for 15% of the time, Pallas kernels for 0%

commit v1 on v0

--- a/solution.py
+++ b/solution.py
@@ -8,6 +8,11 @@
 CAP = 2
 HD = 1024
 EPSILON = 1e-05
+
+
+def swapped_in(x, axis, dim):
+    stack = jnp.stack([x] * lax.axis_size(axis))
+    return jnp.concatenate(lax.all_to_all(stack, axis, 0, 0), axis=dim)
 
 
 def items_in_groups(x, axis, split_dim, concat_dim, work, item_dim, out_dim):
@@ -162,11 +167,7 @@
         * attn_gain.astype(jnp.float32)
         * activated[3]
     ).astype(jnp.bfloat16)
-    partial_out = jnp.dot(
-        gated,
-        lax.all_gather(w_o, "routers", axis=1, tiled=True),
-        preferred_element_type=jnp.float32,
-    )
+    partial_out = jnp.dot(gated, swapped_in(w_o, "routers", 1), preferred_element_type=jnp.float32)
     head_share = sent_and_summed(partial_out, "heads", 1)
     share_cols = head_share.shape[1]
     offset = lax.axis_index("heads") * share_cols

time: 431 us -> 442 us (1.026)
    all_to_all x2, waiting for transfers between devices: 13.6 us -> 58.3 us  [serve_slots(): lax.all_to_all(attended_slots.reshape(sources, per_source, block_width, h...]
    all_gather x1 -> x0, waiting for transfers between devices: 41.3 us -> none  [local(): lax.all_gather(w_o, 'routers', axis=1, tiled=True)]
    all_to_all x0 -> x1, starting transfers between devices: none -> 4.42 us  [swapped_in(): return jnp.concatenate(lax.all_to_all(stack, axis, 0, 0), axis=dim)]
  transfers between devices with their start and end apart: 8 -> 8, of which waited for: 7 -> 6; matrix products, arithmetic and copies ran while one was open for 15% -> 18% of each run, Pallas kernels for 0% -> 0%
where the time goes in v1:
time: 442 us; the launch traced here: 440 us
  waiting for transfers between devices  197 us (45%)
  starting transfers between devices  100 us (23%)
  local copies, waits for them, and re-layouts  40.8 us (9%)
  other arithmetic  37.5 us (8%)
  blocking collectives  28 us (6%)
  matrix products  21.7 us (5%)
  between operations  15.1 us (3%)
    all_to_all x4, waiting for transfers between devices, moved(): lax.all_to_all(group, axis, split_axis=split_dim, concat_axis=concat_dim,...  82.6 us
    all_to_all x4, starting transfers between devices, moved(): lax.all_to_all(group, axis, split_axis=split_dim, concat_axis=concat_dim,...  69 us
    all_to_all x2, waiting for transfers between devices, serve_slots(): lax.all_to_all(attended_slots.reshape(sources, per_source, block_width, h...  58.3 us
    all_gather x1, waiting for transfers between devices, local(): lax.all_gather(w_in, 'routers', axis=1, tiled=True)  55.9 us
    all_to_all x2, starting transfers between devices, serve_slots(): lax.all_to_all(attended_slots.reshape(sources, per_source, block_width, h...  26.7 us
    all_to_all x1, blocking collectives, sent_and_summed(): lax.all_to_all(tiles, axis, split_axis=0, concat_axis=0, tiled=True)  12.2 us
    gather x5, local copies, waits for them, and re-layouts, local(): jnp.take(returned.reshape(slot_count, block_width * half_width), position...  8.96 us
  transfers between devices with their start and end apart: 8, of which 6 were waited for; matrix products, arithmetic and copies ran while one was open for 18% of the time, Pallas kernels for 0%

profile of v1, /device:TPU:65, one launch (start us, length us, event | category | flops | bytes accessed | tf_op | source)
XLA Modules:
  0.0 440.2 jit_solution(1906802080212376735)
XLA Ops:
  6.6 2.1 copy.77
  11.2 44.2 %all-to-all-start.3 = ((s32[16,1,1]{2,1,0:T(1,128)}), s32[16,1,1]{2,1,0:T(1,128)S(1)}, u32[]{:S(2)}, u32[]{:S(2)}) async-start(s32[16,1,1]{2,1,0:T(1,128)} %bitcast.11), calls=%async_computation.3 | async-start | bytes 16384 | tf_op jit(solution)/shard_map/all_to_all | solution.py:21
  55.4 55.9 %all-gather.2.cloned.1.call-done = bf16[4,1024,512]{1,2,0:T(8,128)(2,1)} async-done(((bf16[4,128,512]{1,2,0:T(8,128)(2,1)}), bf16[4,1024,512]{1,2,0:T(8,128)(2,1)}) %all-gather.2.cloned.1.call-update) | async-done | bytes 4194320 | tf_op jit(solution)/shard_map/all_gather | solution.py:97
  111.3 7.8 %bitcast_multiply_fusion = f32[4,1024,512]{1,2,0:T(8,128)S(1)} fusion(bf16[4,1024,512]{1,2,0:T(8,128)(2,1)} %all-gather.2.cloned.1.call-done, bf16[1024,1024,1]{1,0,2:T(8,128)(2,1)} %bitcast.175), kind=kOutput, calls=%fused_computation.54 | convolution fusion | flops 4303355904 | bytes 14680064 | tf_op jit(solution)/shard_map/rk,pkc->prc/dot_general | solution.py:94
  119.1 3.2 copy-done.3
  122.4 1.9 slice_multiply_fusion.1
  126.9 9.9 %all-to-all-start = ((s32[16,1,1]{2,1,0:T(1,128)}), s32[16,1,1]{2,1,0:T(1,128)S(1)}, u32[]{:S(2)}, u32[]{:S(2)}) async-start(s32[16,1,1]{2,1,0:T(1,128)} %bitcast.6), calls=%async_computation | async-start | bytes 16384 | tf_op jit(solution)/shard_map/all_to_all | solution.py:21
  136.8 1.5 fusion.58
  138.2 9.6 %all-to-all-done = s32[16,1,1]{2,1,0:T(1,128)S(1)} async-done(((s32[16,1,1]{2,1,0:T(1,128)}), s32[16,1,1]{2,1,0:T(1,128)S(1)}, u32[]{:S(2)}, u32[]{:S(2)}) %all-to-all-start) | async-done | bytes 96 | tf_op jit(solution)/shard_map/all_to_all | solution.py:21
  147.8 4.1 all-to-all-start.4
  161.9 35.7 %all-to-all-done.4 = bf16[16,1,64,512]{3,2,1,0:T(8,128)(2,1)S(1)} async-done(((bf16[16,1,64,512]{3,2,1,0:T(8,128)(2,1)}), bf16[16,1,64,512]{3,2,1,0:T(8,128)(2,1)S(1)}, u32[]{:S(2)}, u32[]{:S(2)}) %all-to-all-start.4) | async-done | bytes 1048608 | tf_op jit(solution)/shard_map/all_to_all | solution.py:21
  197.6 10.8 %all-to-all-start.1 = ((bf16[16,1,64,512]{3,2,1,0:T(8,128)(2,1)}), bf16[16,1,64,512]{3,2,1,0:T(8,128)(2,1)}, u32[]{:S(2)}, u32[]{:S(2)}) async-start(bf16[16,1,64,512]{3,2,1,0:T(8,128)(2,1)} %get-tuple-element.142), calls=%async_computation.1 | async-start | bytes 2097152 | tf_op jit(solution)/shard_map/all_to_all | solution.py:21
  208.4 1.8 gather_fusion.9
  212.6 1.8 gather_fusion.10
  215.5 37.3 %all-to-all-done.1 = bf16[16,1,64,512]{3,2,1,0:T(8,128)(2,1)} async-done(((bf16[16,1,64,512]{3,2,1,0:T(8,128)(2,1)}), bf16[16,1,64,512]{3,2,1,0:T(8,128)(2,1)}, u32[]{:S(2)}, u32[]{:S(2)}) %all-to-all-start.1) | async-done | bytes 1048608 | tf_op jit(solution)/shard_map/all_to_all | solution.py:21
  252.8 13.8 %all-to-all-start.5 = ((bf16[16,1,64,512]{3,2,1,0:T(8,128)(2,1)}), bf16[16,1,64,512]{3,2,1,0:T(8,128)(2,1)}, u32[]{:S(2)}, u32[]{:S(2)}) async-start(bf16[16,1,64,512]{3,2,1,0:T(8,128)(2,1)} %select_bitcast_fusion.4), calls=%async_computation.5 | async-start | bytes 2097152 | tf_op jit(solution)/shard_map/all_to_all | solution.py:142
  266.6 1.8 gather_fusion.6
  270.7 24.7 %while.20 = (s32[]{:T(128)}, bf16[16,64,512]{2,1,0:T(8,128)(2,1)}, s32[]{:T(128)}, s32[16]{0:T(128)S(1)}, bf16[2,256,512]{2,1,0:T(8,128)(2,1)S(1)}, /*index=5*/b...) while((s32[]{:T(128)}, bf16[16,64,512]{2,1,0:T(8,128)(2,1)}, ...), condition=%wide.region_5.9_spmd, body=%wide.region_4.8_spmd.sunk | while | flops 136971280 | bytes 11538695 | solution.py:137
  271.4 1.6 gather_fusion.1
  273.0 2.8 select_bitcast_fusion.8
  275.8 2.4 fusion.76
  279.7 1.6 gather_fusion.1
  281.3 2.8 select_bitcast_fusion.8
  284.0 2.4 fusion.76
  287.9 1.6 gather_fusion.1
  289.5 2.8 select_bitcast_fusion.8
  292.3 2.4 fusion.76
  295.4 1.8 gather_fusion.7
  298.5 13.3 %all-to-all-done.5 = bf16[16,1,64,512]{3,2,1,0:T(8,128)(2,1)} async-done(((bf16[16,1,64,512]{3,2,1,0:T(8,128)(2,1)}), bf16[16,1,64,512]{3,2,1,0:T(8,128)(2,1)}, u32[]{:S(2)}, u32[]{:S(2)}) %all-to-all-start.5) | async-done | bytes 1048608 | tf_op jit(solution)/shard_map/all_to_all | solution.py:142
  311.8 13.0 %all-to-all-start.2 = ((bf16[16,1,64,512]{3,2,1,0:T(8,128)(2,1)}), bf16[16,1,64,512]{3,2,1,0:T(8,128)(2,1)}, u32[]{:S(2)}, u32[]{:S(2)}) async-start(bf16[16,1,64,512]{3,2,1,0:T(8,128)(2,1)} %select_bitcast_fusion.5), calls=%async_computation.2 | async-start | bytes 2097152 | tf_op jit(solution)/shard_map/all_to_all | solution.py:142
  324.9 45.0 %all-to-all-done.2 = bf16[16,1,64,512]{3,2,1,0:T(8,128)(2,1)} async-done(((bf16[16,1,64,512]{3,2,1,0:T(8,128)(2,1)}), bf16[16,1,64,512]{3,2,1,0:T(8,128)(2,1)}, u32[]{:S(2)}, u32[]{:S(2)}) %all-to-all-start.2) | async-done | bytes 1048608 | tf_op jit(solution)/shard_map/all_to_all | solution.py:142
  371.1 4.4 %all-to-all-start.6 = ((bf16[8,512,128]{1,2,0:T(8,128)(2,1)}), bf16[8,512,128]{1,2,0:T(8,128)(2,1)}, u32[]{:S(2)}, u32[]{:S(2)}) async-start(bf16[8,512,128]{1,2,0:T(8,128)(2,1)} %stack.2), calls=%async_computation.6 | async-start | bytes 2097152 | tf_op jit(solution)/shard_map/all_to_all | solution.py:15
  376.0 1.7 pad_maximum_fusion
  378.9 2.2 gather_fusion.4
  381.2 2.5 gather.19
  384.9 1.5 copy.81
  386.4 1.5 copy.80
  387.9 2.1 fusion.43
  390.0 7.8 %all-reduce = (f32[1024]{0:T(1024)S(1)}, f32[1024]{0:T(1024)S(1)}) all-reduce(f32[1024]{0:T(1024)S(1)} %get-tuple-element.95, f32[1024]{0:T(1024)S(1)} %get-tuple-element.94), channel_id=1, replica_groups=mesh['groups'=2,'users'=16,'routers'=8,'heads'=2] {'heads'}, use_global_device_ids=true, to_apply=%region_16.20 | all-reduce | flops 2048 | bytes 16384 | tf_op jit(solution)/shard_map/psum | solution.py:161
  397.8 2.8 fusion.37
  400.7 2.5 convolution_bitcast_fusion
  403.2 12.2 %all_to_all.53 = f32[2,1024,512]{2,1,0:T(8,128)} all-to-all(f32[2,1024,512]{2,1,0:T(8,128)S(1)} %convolution_bitcast_fusion), channel_id=1, replica_groups=mesh['groups'=2,'users'=16,'routers'=8,'heads'=2] {'heads'}, dimensions={0} | all-to-all | bytes 8388608 | tf_op jit(solution)/shard_map/all_to_all | solution.py:42
  415.4 2.9 reduce_sum.100
  418.3 1.6 multiply_reduce_fusion
  419.9 2.6 psum.23
  422.4 1.7 fusion.44
  424.3 5.4 %all_to_all.54 = f32[2,1024,256]{2,1,0:T(8,128)S(1)} all-to-all(f32[2,1024,256]{2,1,0:T(8,128)S(1)} %broadcast_in_dim.74), channel_id=1, replica_groups=mesh['groups'=2,'users'=16,'routers'=8,'heads'=2] {'heads'}, dimensions={0} | all-to-all | bytes 4194304 | tf_op jit(solution)/shard_map/all_to_all | solution.py:48
  431.0 1.6 fusion.49
  (105 shorter events, 31.2 us)
Async XLA Ops:
  6.5 415.9 %copy-start = (bf16[1024,256]{1,0:T(8,128)(2,1)S(1)}, bf16[1024,256]{1,0:T(8,128)(2,1)}, u32[]{:S(2)}) copy-start(bf16[1024,256]{1,0:T(8,128)(2,1)} %param.32) | copy-start | bytes 1572868
  6.6 104.8 %all-gather.2.cloned.1.call-start = ((), (), s32[]{:S(2)}) async-start(), calls=%async_computation.9 | async-start | bytes 4718592 | tf_op jit(solution)/shard_map/all_gather | solution.py:97
  11.2 115.7 %all-to-all-start.3 = ((s32[16,1,1]{2,1,0:T(1,128)}), s32[16,1,1]{2,1,0:T(1,128)S(1)}, u32[]{:S(2)}, u32[]{:S(2)}) async-start(s32[16,1,1]{2,1,0:T(1,128)} %bitcast.11), calls=%async_computation.3 | async-start | bytes 16384 | tf_op jit(solution)/shard_map/all_to_all | solution.py:21
  119.1 3.2 copy-start.3
  126.9 20.9 %all-to-all-start = ((s32[16,1,1]{2,1,0:T(1,128)}), s32[16,1,1]{2,1,0:T(1,128)S(1)}, u32[]{:S(2)}, u32[]{:S(2)}) async-start(s32[16,1,1]{2,1,0:T(1,128)} %bitcast.6), calls=%async_computation | async-start | bytes 16384 | tf_op jit(solution)/shard_map/all_to_all | solution.py:21
  147.8 49.8 %all-to-all-start.4 = ((bf16[16,1,64,512]{3,2,1,0:T(8,128)(2,1)}), bf16[16,1,64,512]{3,2,1,0:T(8,128)(2,1)S(1)}, u32[]{:S(2)}, u32[]{:S(2)}) async-start(bf16[16,1,64,512]{3,2,1,0:T(8,128)(2,1)} %get-tuple-element.143), calls=%async_computation.4 | async-start | bytes 2097152 | tf_op jit(solution)/shard_map/all_to_all | solution.py:21
  197.6 10.8 %copy-start.6 = (bf16[16,1,64,512]{3,2,1,0:T(8,128)(2,1)}, bf16[16,1,64,512]{3,2,1,0:T(8,128)(2,1)S(1)}, u32[]{:S(2)}) copy-start(bf16[16,1,64,512]{3,2,1,0:T(8,128)(2,1)S(1)} %all-to-all-done.4) | copy-start | bytes 3145732
  197.6 55.2 %all-to-all-start.1 = ((bf16[16,1,64,512]{3,2,1,0:T(8,128)(2,1)}), bf16[16,1,64,512]{3,2,1,0:T(8,128)(2,1)}, u32[]{:S(2)}, u32[]{:S(2)}) async-start(bf16[16,1,64,512]{3,2,1,0:T(8,128)(2,1)} %get-tuple-element.142), calls=%async_computation.1 | async-start | bytes 2097152 | tf_op jit(solution)/shard_map/all_to_all | solution.py:21
  210.3 2.3 copy-start.1
  210.3 2.2 copy-start.2
  252.8 58.9 %all-to-all-start.5 = ((bf16[16,1,64,512]{3,2,1,0:T(8,128)(2,1)}), bf16[16,1,64,512]{3,2,1,0:T(8,128)(2,1)}, u32[]{:S(2)}, u32[]{:S(2)}) async-start(bf16[16,1,64,512]{3,2,1,0:T(8,128)(2,1)} %select_bitcast_fusion.4), calls=%async_computation.5 | async-start | bytes 2097152 | tf_op jit(solution)/shard_map/all_to_all | solution.py:142
  297.2 27.5 %copy-start.7 = (bf16[512,128]{1,0:T(8,128)(2,1)S(1)}, bf16[512,128]{1,0:T(8,128)(2,1)}, u32[]{:S(2)}) copy-start(bf16[512,128]{1,0:T(8,128)(2,1)} %param.30) | copy-start | bytes 393220
  311.8 58.2 %all-to-all-start.2 = ((bf16[16,1,64,512]{3,2,1,0:T(8,128)(2,1)}), bf16[16,1,64,512]{3,2,1,0:T(8,128)(2,1)}, u32[]{:S(2)}, u32[]{:S(2)}) async-start(bf16[16,1,64,512]{3,2,1,0:T(8,128)(2,1)} %select_bitcast_fusion.5), calls=%async_computation.2 | async-start | bytes 2097152 | tf_op jit(solution)/shard_map/all_to_all | solution.py:142
  324.8 50.7 %copy-start.12 = (bf16[256]{0:T(256)(128)(2,1)S(1)}, bf16[256]{0:T(256)(128)(2,1)}, u32[]{:S(2)}) copy-start(bf16[256]{0:T(256)(128)(2,1)} %param.33) | copy-start | bytes 1540
  324.8 50.8 %copy-start.9 = (bf16[512]{0:T(512)(128)(2,1)S(1)}, bf16[512]{0:T(512)(128)(2,1)}, u32[]{:S(2)}) copy-start(bf16[512]{0:T(512)(128)(2,1)} %param.29) | copy-start | bytes 3076
  324.8 50.8 %copy-start.8 = (s32[16,1]{0,1:T(1,128)S(1)}, s32[16,1]{0,1:T(1,128)}, u32[]{:S(2)}) copy-start(s32[16,1]{0,1:T(1,128)} %param.23) | copy-start | bytes 196
  324.8 50.9 %copy-start.10 = (bf16[1024]{0:T(1024)(128)(2,1)S(1)}, bf16[1024]{0:T(1024)(128)(2,1)}, u32[]{:S(2)}) copy-start(bf16[1024]{0:T(1024)(128)(2,1)} %param.31) | copy-start | bytes 6148
  324.8 51.0 %copy-start.5 = (f32[1,1024,512]{1,2,0:T(8,128)S(1)}, f32[1,1024,512]{1,2,0:T(8,128)}, u32[]{:S(2)}) copy-start(f32[1,1024,512]{1,2,0:T(8,128)} %get-tuple-element.136) | copy-start | bytes 6291460
  371.1 29.6 %all-to-all-start.6 = ((bf16[8,512,128]{1,2,0:T(8,128)(2,1)}), bf16[8,512,128]{1,2,0:T(8,128)(2,1)}, u32[]{:S(2)}, u32[]{:S(2)}) async-start(bf16[8,512,128]{1,2,0:T(8,128)(2,1)} %stack.2), calls=%async_computation.6 | async-start | bytes 2097152 | tf_op jit(solution)/shard_map/all_to_all | solution.py:15
  381.2 2.5 copy-start.4
  431.0 1.7 copy-start.11
Sparse Core Ops, SparseCore 0:
  9.4 101.9 all-gather.1
